TPU v7x, 32 devices: a whole 2x2x4 slice. The times are simulated.
32 devices in a mesh: dom: 16 (over z, y, x), mem: 2 (over core).
Axes of the slice: x: 2, y: 2, z: 4, core: 2. Of those that a mesh axis runs over, the one named last changes fastest.
Arguments:
- node_latents: bfloat16 [4, 2048, 512], P('mem', 'dom'), may hold values from -6 to 6
- edge_latents: bfloat16 [4, 8192, 512], P('mem', 'dom'), may hold values from -6 to 6
- edge_senders: int32 [8192], P('dom'), may hold values from 0 to 191, as said below
- edge_receivers: int32 [8192], P('dom'), may hold values from 0 to 127
- edge_counts: int32 [16], P('dom'), may hold values from 64 to 512, as said below
- halo_send: int32 [512], P('dom'), may hold values from 0 to 127
- long_send: int32 [16, 16, 2], replicated, may hold values from 0 to 3
- edge_first: bfloat16 [2, 1536, 512], P(None, None, 'mem'), may hold values from -0.15625 to 0.15625
- edge_second: bfloat16 [2, 512, 512], P(None, None, 'mem'), may hold values from -0.25 to 0.25
- node_first: bfloat16 [2, 1024, 512], P(None, None, 'mem'), may hold values from -0.1875 to 0.1875
- node_second: bfloat16 [2, 512, 512], P(None, None, 'mem'), may hold values from -0.25 to 0.25
- edge_gain: float32 [2, 512], replicated, may hold values from 0.5 to 1.5
- edge_shift: float32 [2, 512], replicated, may hold values from -3 to 3
- node_gain: float32 [2, 512], replicated, may hold values from 0.5 to 1.5
- node_shift: float32 [2, 512], replicated, may hold values from -3 to 3
Outputs:
- node_out: bfloat16 [4, 2048, 512], P('mem', 'dom')
- edge_out: bfloat16 [4, 8192, 512], P('mem', 'dom')
Inputs may be any that keep to these rules, and one draw needn't show every extreme that they name: `edge_senders`: rows below 128 are the partition's own nodes, the next 32 its neighbours' sent nodes, the rest the coarse slots of all partitions. `edge_counts`: live slots come first in each partition; some partition has exactly 512 live slots.
All inputs are finite; a program needn't handle non-finite values.
Results may differ from a plain program's by a relative error of at most 0.0075.
Values may be sent and summed in bfloat16 or wider, within the bound.
A program may use at most 128 MiB of HBM per device.

v0:
```python
import jax
import jax.numpy as jnp
from jax import lax
from jax.sharding import PartitionSpec as P

HALO = 16
LAYERS = 2


def with_halo(block, sides, width):
    for axis, dim in sides:
        count = lax.axis_size(axis)
        forward = [(i, i + 1) for i in range(count - 1)]
        forward.append((count - 1, 0))
        backward = [(target, source) for source, target in forward]
        low = lax.ppermute(
            lax.slice_in_dim(block, block.shape[dim] - width, None, axis=dim), axis, forward
        )
        high = lax.ppermute(lax.slice_in_dim(block, 0, width, axis=dim), axis, backward)
        block = jnp.concatenate([low, block, high], axis=dim)
    return block


def project_norm(inputs, first_weight, second, scale_gain, offset):
    hidden = jax.nn.silu(jnp.dot(inputs, first_weight, preferred_element_type=jnp.float32)).astype(
        jnp.bfloat16
    )
    output = jnp.dot(hidden, second, preferred_element_type=jnp.float32)
    average = jnp.mean(output, -1, keepdims=True)
    centred = output - average
    variance = jnp.mean(centred * centred, -1, keepdims=True)
    return centred * lax.rsqrt(variance + 1e-05) * scale_gain + offset


def per_device(
    node_latents,
    edge_latents,
    edge_senders,
    edge_receivers,
    edge_counts,
    halo_send,
    long_send,
    edge_first,
    edge_second,
    node_first,
    node_second,
    edge_gain,
    edge_shift,
    node_gain,
    node_shift,
):
    members, node_rows, features = node_latents.shape
    edge_rows = edge_latents.shape[1]
    position = lax.axis_index("dom")
    live_count = edge_counts[0]
    live_mask = jnp.arange(edge_rows, dtype=jnp.int32) < live_count
    onehot = (
        (edge_receivers[None, :] == jnp.arange(node_rows, dtype=jnp.int32)[:, None])
        & live_mask[None, :]
    ).astype(jnp.bfloat16)
    node_state = node_latents
    edge_state = edge_latents
    for layer_index in range(LAYERS):
        edge_inner, edge_outer, node_inner, node_outer = (
            lax.all_gather(edge_first[layer_index], "mem", axis=1, tiled=True),
            lax.all_gather(edge_second[layer_index], "mem", axis=1, tiled=True),
            lax.all_gather(node_first[layer_index], "mem", axis=1, tiled=True),
            lax.all_gather(node_second[layer_index], "mem", axis=1, tiled=True),
        )
        outgoing = jnp.take(node_state, halo_send, axis=1)
        bordered = with_halo(outgoing, (("dom", 1),), HALO)
        from_left = bordered[:, :HALO]
        from_right = bordered[:, 3 * HALO :]
        send_rows = lax.dynamic_index_in_dim(long_send, position, 0, keepdims=False).reshape(-1)
        packed = jnp.take(node_state, send_rows, axis=1)
        far_rows = lax.all_to_all(packed, "dom", split_axis=1, concat_axis=1, tiled=True)
        sources = jnp.concatenate([node_state, from_left, from_right, far_rows], 1)
        sender_rows = jnp.take(sources, edge_senders, axis=1)
        receiver_rows = jnp.take(node_state, edge_receivers, axis=1)
        joined = jnp.concatenate([edge_state, sender_rows, receiver_rows], -1)
        update = project_norm(
            joined.reshape(members * edge_rows, 3 * features),
            edge_inner,
            edge_outer,
            edge_gain[layer_index],
            edge_shift[layer_index],
        ).reshape(members, edge_rows, features)
        new_edges = jnp.where(
            live_mask[None, :, None], edge_state.astype(jnp.float32) + update, 0.0
        ).astype(jnp.bfloat16)
        summed = jnp.einsum(
            "ne,med->mnd", onehot, new_edges, preferred_element_type=jnp.float32
        ).astype(jnp.bfloat16)
        node_in = jnp.concatenate([node_state, summed], -1).reshape(
            members * node_rows, 2 * features
        )
        node_update = project_norm(
            node_in, node_inner, node_outer, node_gain[layer_index], node_shift[layer_index]
        ).reshape(members, node_rows, features)
        node_state = (node_state.astype(jnp.float32) + node_update).astype(jnp.bfloat16)
        edge_state = new_edges
    return (node_state, edge_state)


def solution(mesh):
    placed = (
        P("mem", "dom", None),
        P("mem", "dom", None),
        P("dom"),
        P("dom"),
        P("dom"),
        P("dom"),
        P(),
        P(None, None, "mem"),
        P(None, None, "mem"),
        P(None, None, "mem"),
        P(None, None, "mem"),
        P(),
        P(),
        P(),
        P(),
    )
    return jax.shard_map(
        per_device,
        mesh=mesh,
        in_specs=placed,
        out_specs=(P("mem", "dom", None), P("mem", "dom", None)),
        check_vma=False,
    )
```

profile of v0, /device:TPU:0, one launch (start us, length us, event | category | flops | bytes accessed | tf_op | source)
XLA Modules:
  0.0 136.8 jit_solution(4153508605069682487)
XLA Ops:
  7.2 2.7 %fusion.60 = (bf16[1,1536,256]{2,1,0:T(8,128)(2,1)}, bf16[1,1536,256]{2,1,0:T(8,128)(2,1)}) fusion(bf16[2,1536,256]{2,1,0:T(8,128)(2,1)} %param.28), kind=kLoop, calls=%fused_computation.105 | loop fusion | bytes 3145728 | tf_op jit(solution)/shard_map/slice | solution.py:65
  10.1 1.1 fusion.61
  11.2 0.7 all-gather.17.cloned.1.call-update
  12.2 0.8 gather_fusion.1
  13.0 0.7 copy.84
  13.7 8.3 %all-to-all-start = ((bf16[2,32,512]{2,0,1:T(2,128)(2,1)}), bf16[2,32,512]{2,0,1:T(2,128)(2,1)S(1)}, u32[]{:S(2)}, u32[]{:S(2)}) async-start(bf16[2,32,512]{2,0,1:T(2,128)(2,1)} %copy.84), calls=%async_computation | async-start | bytes 131072 | tf_op jit(solution)/shard_map/all_to_all | solution.py:76
  22.2 0.8 gather_fusion
  23.0 2.0 %collective-permute-start = (bf16[2,16,512]{2,1,0:T(8,128)(2,1)S(1)}, bf16[2,16,512]{2,1,0:T(8,128)(2,1)S(1)}, u32[]{:S(2)}, u32[]{:S(2)}) collective-permute-start(bf16[2,16,512]{2,1,0:T(8,128)(2,1)S(1)} %get-tuple-element.23), channel_id=1, source_target_pairs={{0,2},{2,4},{4,6},{6,8},{8,10},{10,12},{12,14},{14,16},{16,18},{18... | collective-permute-start | bytes 98312 | tf_op jit(solution)/shard_map/ppermute | solution.py:16
  25.0 3.7 %collective-permute-start.1 = (bf16[2,16,512]{2,1,0:T(8,128)(2,1)S(1)}, bf16[2,16,512]{2,1,0:T(8,128)(2,1)S(1)}, u32[]{:S(2)}, u32[]{:S(2)}) collective-permute-start(bf16[2,16,512]{2,1,0:T(8,128)(2,1)S(1)} %get-tuple-element.24), channel_id=1, source_target_pairs={{2,0},{4,2},{6,4},{8,6},{10,8},{12,10},{14,12},{16,14},{18,16},{20... | collective-permute-start | bytes 98312 | tf_op jit(solution)/shard_map/ppermute | solution.py:19
  28.9 4.4 %gather_fusion.3 = bf16[512,2,512]{2,0,1:T(8,128)(2,1)S(1)} fusion(bf16[2,128,512]{2,1,0:T(8,128)(2,1)S(1)} %copy-done.1, s32[1024]{0:T(1024)S(1)} %pad_clamp_fusion), kind=kCustom, calls=%fused_computation.2.clone | custom fusion | bytes 2099200 | tf_op jit(solution)/shard_map/jit(_take)/gather | solution.py:79
  33.4 2.4 %all-gather.1 = bf16[1,512,512]{2,1,0:T(8,128)(2,1)} all-gather(bf16[1,512,256]{2,1,0:T(8,128)(2,1)S(1)} %get-tuple-element.18), channel_id=3, replica_groups=mesh['dom'=16,'mem'=2] {'mem'}, dimensions={2}, use_global_device_ids=true | all-gather | bytes 786432 | tf_op jit(solution)/shard_map/all_gather | solution.py:66
  35.9 2.3 %all-gather.3 = bf16[1,512,512]{2,1,0:T(8,128)(2,1)} all-gather(bf16[1,512,256]{2,1,0:T(8,128)(2,1)S(1)} %get-tuple-element.19), channel_id=5, replica_groups=mesh['dom'=16,'mem'=2] {'mem'}, dimensions={2}, use_global_device_ids=true | all-gather | bytes 786432 | tf_op jit(solution)/shard_map/all_gather | solution.py:68
  38.3 2.3 %all-gather.5 = bf16[1,512,512]{2,1,0:T(8,128)(2,1)} all-gather(bf16[1,512,256]{2,1,0:T(8,128)(2,1)S(1)} %get-tuple-element.17), channel_id=7, replica_groups=mesh['dom'=16,'mem'=2] {'mem'}, dimensions={2}, use_global_device_ids=true | all-gather | bytes 786432 | tf_op jit(solution)/shard_map/all_gather | solution.py:66
  40.6 2.6 %all-gather.7 = bf16[1,512,512]{2,1,0:T(8,128)(2,1)} all-gather(bf16[1,512,256]{2,1,0:T(8,128)(2,1)S(1)} %get-tuple-element.20), channel_id=9, replica_groups=mesh['dom'=16,'mem'=2] {'mem'}, dimensions={2}, use_global_device_ids=true | all-gather | bytes 786432 | tf_op jit(solution)/shard_map/all_gather | solution.py:68
  43.2 5.0 %fusion.29 = bf16[2,512,512]{2,0,1:T(2,128)(2,1)} fusion(bf16[512,2,512]{2,0,1:T(8,128)(2,1)S(1)} %gather_fusion.3, pred[512]{0:T(512)(128)(4,1)S(1)} %compare_and_fusion), kind=kLoop, calls=%fused_computation.45 | loop fusion | flops 524288 | bytes 2097664 | tf_op jit(solution)/shard_map/jit(_take)/select_n | solution.py:79
  48.8 0.3 copy.85
  49.1 0.2 copy.81
  49.3 2.1 %copy.82 = bf16[2,512,512]{2,0,1:T(2,128)(2,1)} copy(bf16[2,512,512]{2,1,0:T(8,128)(2,1)S(1)} %copy-done.2) | data formatting | bytes 2097152 | tf_op args[1]
  51.5 0.6 pad_maximum_fusion.5
  52.1 3.6 %gather_fusion.2 = bf16[512,2,512]{2,1,0:T(2,128)(2,1)S(1)} fusion(bf16[2,192,512]{2,0,1:T(2,128)(2,1)S(1)} %pad_maximum_fusion.5, s32[1024]{0:T(1024)S(1)} %pad_clamp_fusion.1), kind=kCustom, calls=%fused_computation.1.clone | custom fusion | bytes 2099200 | tf_op jit(solution)/shard_map/jit(_take)/gather | solution.py:78
  55.7 2.0 %fusion.27 = bf16[2,512,512]{2,0,1:T(2,128)(2,1)S(1)} fusion(bf16[512,2,512]{2,1,0:T(2,128)(2,1)S(1)} %gather_fusion.2, pred[512]{0:T(512)(128)(4,1)S(1)} %compare_and_fusion.1), kind=kLoop, calls=%fused_computation.43 | loop fusion | flops 524288 | bytes 2097664 | tf_op jit(solution)/shard_map/jit(_take)/select_n | solution.py:78
  57.7 3.3 %pad_maximum_fusion = bf16[2,512,1536]{2,0,1:T(2,128)(2,1)S(1)} fusion(bf16[2,512,512]{2,0,1:T(2,128)(2,1)S(1)} %copy-done.4, bf16[2,512,512]{2,0,1:T(2,128)(2,1)S(1)} %fusion.27, bf16[2,512,512]{2,0,1:T(2,128)(2,1)S(1)} %copy-done.6), kind=kLoop, calls=%fused_computation.8 | loop fusion | flops 9437184 | bytes 6291456 | tf_op jit(solution)/shard_map/concatenate | solution.py:80
  61.0 2.1 %copy.90 = bf16[2,512,1536]{2,1,0:T(8,128)(2,1)} copy(bf16[2,512,1536]{2,0,1:T(2,128)(2,1)S(1)} %pad_maximum_fusion) | data formatting | bytes 6291456 | tf_op jit(solution)/shard_map/concatenate | solution.py:80
  63.1 5.0 %fusion.70 = (f32[1024]{0:T(1024)S(1)}, f32[1024,512]{1,0:T(8,128)S(1)}) fusion(bf16[1,512,512]{2,1,0:T(8,128)(2,1)} %all-gather.1, bf16[1024,1536]{1,0:T(8,128)(2,1)} %bitcast.105, bf16[1,1536,512]{2,1,0:T(8,128)(2,1)} %all-gather.13.cloned.1.call-done), kind=kOutput, calls=%fused_computation.115 | convolution fusion | flops 2150628352 | bytes 7344128 | tf_op jit(solution)/shard_map/dot_general | solution.py:28
  68.1 0.4 multiply_reduce_fusion.1
  68.5 0.4 multiply_add_fusion.1
  68.9 5.5 %fusion.3 = bf16[2,512,512]{2,0,1:T(2,128)(2,1)S(1)} fusion(f32[2,512,512]{2,1,0:T(8,128)S(1)} %bitcast.104, pred[512]{0:T(512)(128)(4,1)S(1)} %iota_compare_fusion.1, bf16[2,512,512]{2,1,0:T(8,128)(2,1)S(1)} %copy-done.2), kind=kLoop, calls=%fused_computation.15 | loop fusion | flops 2097152 | bytes 4194816 | tf_op jit(solution)/shard_map/convert_element_type | solution.py:90
  74.4 0.5 fusion.18
  75.0 0.2 copy.94
  75.2 0.2 copy-done.11
  75.5 2.0 %fusion.73 = (f32[256]{0:T(256)S(1)}, f32[256,512]{1,0:T(8,128)S(1)}) fusion(bf16[1,512,512]{2,1,0:T(8,128)(2,1)S(1)} %copy-done.11, bf16[256,1024]{1,0:T(8,128)(2,1)S(1)} %bitcast.109, bf16[1,1024,512]{2,1,0:T(8,128)(2,1)} %all-gather.15.cloned.1.call-done), kind=kOutput, calls=%fused_computation.116 | convolution fusion | flops 403439360 | bytes 2622464 | tf_op jit(solution)/shard_map/dot_general | solution.py:28
  77.5 0.2 multiply_reduce_fusion.3
  77.9 0.2 copy.95
  78.1 0.4 copy-done.8
  78.5 0.2 copy.96
  78.7 0.7 gather_fusion.4
  79.4 0.7 gather_fusion.5
  80.1 3.6 %gather_fusion.7 = bf16[512,2,512]{2,1,0:T(2,128)(2,1)S(1)} fusion(bf16[2,128,512]{2,0,1:T(2,128)(2,1)S(1)} %copy.96, s32[1024]{0:T(1024)S(1)} %pad_clamp_fusion), kind=kCustom, calls=%fused_computation.7.clone | custom fusion | bytes 2099200 | tf_op jit(solution)/shard_map/jit(_take)/gather | solution.py:79
  83.6 0.2 copy.97
  83.9 0.8 fusion.64
  84.7 5.6 %collective-permute-start.3 = (bf16[2,16,512]{1,2,0:T(8,128)(2,1)S(1)}, bf16[2,16,512]{1,2,0:T(8,128)(2,1)}, u32[]{:S(2)}, u32[]{:S(2)}) collective-permute-start(bf16[2,16,512]{1,2,0:T(8,128)(2,1)S(1)} %get-tuple-element.22), channel_id=1, source_target_pairs={{2,0},{4,2},{6,4},{8,6},{10,8},{12,10},{14,12},{16,14},{18,16},{20... | collective-permute-start | bytes 98312 | tf_op jit(solution)/shard_map/ppermute | solution.py:19
  90.3 0.7 fusion.55
  91.1 3.5 %all-to-all-start.1 = ((bf16[2,32,512]{2,0,1:T(2,128)(2,1)}), bf16[2,32,512]{2,0,1:T(2,128)(2,1)S(1)}, u32[]{:S(2)}, u32[]{:S(2)}) async-start(bf16[2,32,512]{2,0,1:T(2,128)(2,1)} %fusion.55), calls=%async_computation.1 | async-start | bytes 131072 | tf_op jit(solution)/shard_map/all_to_all | solution.py:76
  94.6 2.6 %fusion.30 = bf16[2,512,512]{2,0,1:T(2,128)(2,1)} fusion(bf16[512,2,512]{2,1,0:T(2,128)(2,1)S(1)} %gather_fusion.7, pred[512]{0:T(512)(128)(4,1)S(1)} %compare_and_fusion), kind=kLoop, calls=%fused_computation.46 | loop fusion | flops 524288 | bytes 2097664 | tf_op jit(solution)/shard_map/jit(_take)/select_n | solution.py:79
  97.2 4.9 %all-to-all-done.1 = bf16[2,32,512]{2,0,1:T(2,128)(2,1)S(1)} async-done(((bf16[2,32,512]{2,0,1:T(2,128)(2,1)}), bf16[2,32,512]{2,0,1:T(2,128)(2,1)S(1)}, u32[]{:S(2)}, u32[]{:S(2)}) %all-to-all-start.1) | async-done | bytes 65568 | tf_op jit(solution)/shard_map/all_to_all | solution.py:76
  102.1 0.2 copy.99
  102.3 1.2 pad_maximum_fusion.3
  103.5 0.5 copy.100
  104.0 3.6 %gather_fusion.6 = bf16[512,2,512]{2,1,0:T(2,128)(2,1)S(1)} fusion(bf16[2,192,512]{2,0,1:T(2,128)(2,1)S(1)} %copy.100, s32[1024]{0:T(1024)S(1)} %pad_clamp_fusion.1), kind=kCustom, calls=%fused_computation.6.clone | custom fusion | bytes 2099200 | tf_op jit(solution)/shard_map/jit(_take)/gather | solution.py:78
  107.6 2.0 %fusion.28 = bf16[2,512,512]{2,0,1:T(2,128)(2,1)S(1)} fusion(bf16[512,2,512]{2,1,0:T(2,128)(2,1)S(1)} %gather_fusion.6, pred[512]{0:T(512)(128)(4,1)S(1)} %compare_and_fusion.1), kind=kLoop, calls=%fused_computation.44 | loop fusion | flops 524288 | bytes 2097664 | tf_op jit(solution)/shard_map/jit(_take)/select_n | solution.py:78
  109.6 3.3 %pad_maximum_fusion.1 = bf16[2,512,1536]{2,0,1:T(2,128)(2,1)S(1)} fusion(bf16[2,512,512]{2,0,1:T(2,128)(2,1)S(1)} %copy-done.5, bf16[2,512,512]{2,0,1:T(2,128)(2,1)S(1)} %fusion.28, bf16[2,512,512]{2,0,1:T(2,128)(2,1)S(1)} %fusion.3), kind=kLoop, calls=%fused_computation.9 | loop fusion | flops 9437184 | bytes 6291456 | tf_op jit(solution)/shard_map/concatenate | solution.py:80
  112.9 2.1 %copy.102 = bf16[2,512,1536]{2,1,0:T(8,128)(2,1)} copy(bf16[2,512,1536]{2,0,1:T(2,128)(2,1)S(1)} %pad_maximum_fusion.1) | data formatting | bytes 6291456 | tf_op jit(solution)/shard_map/concatenate | solution.py:80
  115.0 5.0 %fusion.76 = (f32[1024]{0:T(1024)S(1)}, f32[1024,512]{1,0:T(8,128)S(1)}) fusion(bf16[1,512,512]{2,1,0:T(8,128)(2,1)} %all-gather.5, bf16[1024,1536]{1,0:T(8,128)(2,1)} %bitcast.106, bf16[1,1536,512]{2,1,0:T(8,128)(2,1)} %all-gather.17.cloned.1.call-done), kind=kOutput, calls=%fused_computation.117 | convolution fusion | flops 2150628352 | bytes 7344128 | tf_op jit(solution)/shard_map/dot_general | solution.py:28
  120.0 0.4 multiply_reduce_fusion
  120.4 0.4 multiply_add_fusion
  120.8 4.3 %fusion.1 = bf16[2,512,512]{2,0,1:T(2,128)(2,1)S(1)} fusion(f32[2,512,512]{2,1,0:T(8,128)S(1)} %bitcast.103, bf16[2,512,512]{2,0,1:T(2,128)(2,1)S(1)} %fusion.3, pred[512]{0:T(512)(128)(4,1)S(1)} %iota_compare_fusion.1), kind=kLoop, calls=%fused_computation.12 | loop fusion | flops 2097152 | bytes 4194816 | tf_op jit(solution)/shard_map/convert_element_type | solution.py:90
  125.1 0.2 copy.108
  125.3 0.5 fusion.19
  125.8 0.2 copy.105
  126.1 0.6 copy-done.10
  126.7 2.0 %fusion.79 = (f32[256]{0:T(256)S(1)}, f32[256,512]{1,0:T(8,128)S(1)}) fusion(bf16[1,512,512]{2,1,0:T(8,128)(2,1)S(1)} %copy-done.10, bf16[256,1024]{1,0:T(8,128)(2,1)S(1)} %bitcast.110, bf16[1,1024,512]{2,1,0:T(8,128)(2,1)} %all-gather.19.cloned.1.call-done), kind=kOutput, calls=%fused_computation.118 | convolution fusion | flops 403439360 | bytes 2622464 | tf_op jit(solution)/shard_map/dot_general | solution.py:28
  128.7 0.2 multiply_reduce_fusion.2
  129.1 0.2 copy.106
  129.4 0.8 copy.107
  (98 shorter events, 1.5 us)
Async XLA Ops:
  7.2 4.8 %copy-start = (s32[16,16,2]{1,2,0:T(2,128)S(1)}, s32[16,16,2]{1,2,0:T(2,128)}, u32[]{:S(2)}) copy-start(s32[16,16,2]{1,2,0:T(2,128)} %param.27) | copy-start | bytes 6148
  7.2 2.9 %copy-start.9 = (bf16[2,1024,256]{2,1,0:T(8,128)(2,1)S(1)}, bf16[2,1024,256]{2,1,0:T(8,128)(2,1)}, u32[]{:S(2)}) copy-start(bf16[2,1024,256]{2,1,0:T(8,128)(2,1)} %param.30) | copy-start | bytes 3145732
  7.2 55.9 %all-gather.13.cloned.1.call-start = ((), (), s32[]{:S(2)}) async-start(), calls=%async_computation.2 | async-start | bytes 2359296 | tf_op jit(solution)/shard_map/all_gather | solution.py:65
  10.0 2.2 %copy-start.1 = (bf16[2,128,512]{2,1,0:T(8,128)(2,1)S(1)}, bf16[2,128,512]{2,1,0:T(8,128)(2,1)}, u32[]{:S(2)}) copy-start(bf16[2,128,512]{2,1,0:T(8,128)(2,1)} %param.21) | copy-start | bytes 786436
  10.0 12.1 %copy-start.20 = (s32[32]{0:T(128)S(1)}, s32[32]{0:T(128)}, u32[]{:S(2)}) copy-start(s32[32]{0:T(128)} %param.26) | copy-start | bytes 388
  10.0 65.2 %all-gather.15.cloned.1.call-start = ((), (), s32[]{:S(2)}) async-start(), calls=%async_computation.3 | async-start | bytes 1572864 | tf_op jit(solution)/shard_map/all_gather | solution.py:67
  11.2 17.6 %copy-start.15 = (s32[512]{0:T(512)S(1)}, s32[512]{0:T(512)}, u32[]{:S(2)}) copy-start(s32[512]{0:T(512)} %param.23) | copy-start | bytes 6148
  11.2 17.6 %copy-start.14 = (s32[512]{0:T(512)S(1)}, s32[512]{0:T(512)}, u32[]{:S(2)}) copy-start(s32[512]{0:T(512)} %param.24) | copy-start | bytes 6148
  11.2 103.8 %all-gather.17.cloned.1.call-start = ((), (), s32[]{:S(2)}) async-start(), calls=%async_computation.4 | async-start | bytes 2359296 | tf_op jit(solution)/shard_map/all_gather | solution.py:65
  13.7 37.8 %all-to-all-start = ((bf16[2,32,512]{2,0,1:T(2,128)(2,1)}), bf16[2,32,512]{2,0,1:T(2,128)(2,1)S(1)}, u32[]{:S(2)}, u32[]{:S(2)}) async-start(bf16[2,32,512]{2,0,1:T(2,128)(2,1)} %copy.84), calls=%async_computation | async-start | bytes 131072 | tf_op jit(solution)/shard_map/all_to_all | solution.py:76
  22.1 104.0 %all-gather.19.cloned.1.call-start = ((), (), s32[]{:S(2)}) async-start(), calls=%async_computation.5 | async-start | bytes 1572864 | tf_op jit(solution)/shard_map/all_gather | solution.py:67
  23.0 28.3 %collective-permute-start = (bf16[2,16,512]{2,1,0:T(8,128)(2,1)S(1)}, bf16[2,16,512]{2,1,0:T(8,128)(2,1)S(1)}, u32[]{:S(2)}, u32[]{:S(2)}) collective-permute-start(bf16[2,16,512]{2,1,0:T(8,128)(2,1)S(1)} %get-tuple-element.23), channel_id=1, source_target_pairs={{0,2},{2,4},{4,6},{6,8},{8,10},{10,12},{12,14},{14,16},{16,18},{18... | collective-permute-start | bytes 98312 | tf_op jit(solution)/shard_map/ppermute | solution.py:16
  25.0 26.4 %collective-permute-start.1 = (bf16[2,16,512]{2,1,0:T(8,128)(2,1)S(1)}, bf16[2,16,512]{2,1,0:T(8,128)(2,1)S(1)}, u32[]{:S(2)}, u32[]{:S(2)}) collective-permute-start(bf16[2,16,512]{2,1,0:T(8,128)(2,1)S(1)} %get-tuple-element.24), channel_id=1, source_target_pairs={{2,0},{4,2},{6,4},{8,6},{10,8},{12,10},{14,12},{16,14},{18,16},{20... | collective-permute-start | bytes 98312 | tf_op jit(solution)/shard_map/ppermute | solution.py:19
  28.8 4.5 %copy-start.12 = (bf16[2,512,256]{2,1,0:T(8,128)(2,1)S(1)}, bf16[2,512,256]{2,1,0:T(8,128)(2,1)}, u32[]{:S(2)}) copy-start(bf16[2,512,256]{2,1,0:T(8,128)(2,1)} %param.29) | copy-start | bytes 1572868
  28.8 7.0 %copy-start.16 = (f32[2,512]{1,0:T(2,128)S(1)}, f32[2,512]{1,0:T(2,128)}, u32[]{:S(2)}) copy-start(f32[2,512]{1,0:T(2,128)} %param.32) | copy-start | bytes 12292
  28.8 7.0 %copy-start.17 = (f32[2,512]{1,0:T(2,128)S(1)}, f32[2,512]{1,0:T(2,128)}, u32[]{:S(2)}) copy-start(f32[2,512]{1,0:T(2,128)} %param.33) | copy-start | bytes 12292
  33.3 2.6 %copy-start.13 = (bf16[2,512,256]{2,1,0:T(8,128)(2,1)S(1)}, bf16[2,512,256]{2,1,0:T(8,128)(2,1)}, u32[]{:S(2)}) copy-start(bf16[2,512,256]{2,1,0:T(8,128)(2,1)} %param.31) | copy-start | bytes 1572868
  33.3 4.9 %copy-start.18 = (f32[2,512]{1,0:T(2,128)S(1)}, f32[2,512]{1,0:T(2,128)}, u32[]{:S(2)}) copy-start(f32[2,512]{1,0:T(2,128)} %param.34) | copy-start | bytes 12292
  33.3 4.9 %copy-start.19 = (f32[2,512]{1,0:T(2,128)S(1)}, f32[2,512]{1,0:T(2,128)}, u32[]{:S(2)}) copy-start(f32[2,512]{1,0:T(2,128)} %param.35) | copy-start | bytes 12292
  40.6 8.7 %copy-start.2 = (bf16[2,512,512]{2,1,0:T(8,128)(2,1)S(1)}, bf16[2,512,512]{2,1,0:T(8,128)(2,1)}, u32[]{:S(2)}) copy-start(bf16[2,512,512]{2,1,0:T(8,128)(2,1)} %param.22) | copy-start | bytes 3145732
  49.3 25.6 %copy-start.7 = (bf16[2,128,512]{1,2,0:T(8,128)(2,1)}, bf16[2,128,512]{1,2,0:T(8,128)(2,1)S(1)}, u32[]{:S(2)}) copy-start(bf16[2,128,512]{1,2,0:T(8,128)(2,1)S(1)} %copy.81) | copy-start | bytes 786436
  55.6 2.0 %copy-start.4 = (bf16[2,512,512]{2,0,1:T(2,128)(2,1)S(1)}, bf16[2,512,512]{2,0,1:T(2,128)(2,1)}, u32[]{:S(2)}) copy-start(bf16[2,512,512]{2,0,1:T(2,128)(2,1)} %fusion.29) | copy-start | bytes 3145732
  55.7 2.0 %copy-start.6 = (bf16[2,512,512]{2,0,1:T(2,128)(2,1)S(1)}, bf16[2,512,512]{2,0,1:T(2,128)(2,1)}, u32[]{:S(2)}) copy-start(bf16[2,512,512]{2,0,1:T(2,128)(2,1)} %copy.82) | copy-start | bytes 3145732
  74.4 1.0 copy-start.11
  77.5 1.0 copy-start.8
  84.7 17.6 %collective-permute-start.2 = (bf16[2,16,512]{1,2,0:T(8,128)(2,1)}, bf16[2,16,512]{1,2,0:T(8,128)(2,1)S(1)}, u32[]{:S(2)}, u32[]{:S(2)}) collective-permute-start(bf16[2,16,512]{1,2,0:T(8,128)(2,1)} %get-tuple-element.21), channel_id=1, source_target_pairs={{0,2},{2,4},{4,6},{6,8},{8,10},{10,12},{12,14},{14,16},{16,18},{18... | collective-permute-start | bytes 98312 | tf_op jit(solution)/shard_map/ppermute | solution.py:16
  84.7 17.6 %collective-permute-start.3 = (bf16[2,16,512]{1,2,0:T(8,128)(2,1)S(1)}, bf16[2,16,512]{1,2,0:T(8,128)(2,1)}, u32[]{:S(2)}, u32[]{:S(2)}) collective-permute-start(bf16[2,16,512]{1,2,0:T(8,128)(2,1)S(1)} %get-tuple-element.22), channel_id=1, source_target_pairs={{2,0},{4,2},{6,4},{8,6},{10,8},{12,10},{14,12},{16,14},{18,16},{20... | collective-permute-start | bytes 98312 | tf_op jit(solution)/shard_map/ppermute | solution.py:19
  91.1 11.0 %all-to-all-start.1 = ((bf16[2,32,512]{2,0,1:T(2,128)(2,1)}), bf16[2,32,512]{2,0,1:T(2,128)(2,1)S(1)}, u32[]{:S(2)}, u32[]{:S(2)}) async-start(bf16[2,32,512]{2,0,1:T(2,128)(2,1)} %fusion.55), calls=%async_computation.1 | async-start | bytes 131072 | tf_op jit(solution)/shard_map/all_to_all | solution.py:76
  107.6 2.0 %copy-start.5 = (bf16[2,512,512]{2,0,1:T(2,128)(2,1)S(1)}, bf16[2,512,512]{2,0,1:T(2,128)(2,1)}, u32[]{:S(2)}) copy-start(bf16[2,512,512]{2,0,1:T(2,128)(2,1)} %fusion.30) | copy-start | bytes 3145732
  125.3 3.4 %copy-start.3 = (bf16[2,512,512]{2,1,0:T(8,128)(2,1)}, bf16[2,512,512]{2,1,0:T(8,128)(2,1)S(1)}, u32[]{:S(2)}) copy-start(bf16[2,512,512]{2,1,0:T(8,128)(2,1)S(1)} %copy.108) | copy-start | bytes 3145732
  125.3 1.4 %copy-start.10 = (bf16[1,512,512]{2,1,0:T(8,128)(2,1)S(1)}, bf16[1,512,512]{2,1,0:T(8,128)(2,1)}, u32[]{:S(2)}) copy-start(bf16[1,512,512]{2,1,0:T(8,128)(2,1)} %all-gather.7) | copy-start | bytes 1572868
Sparse Core Ops, SparseCore 0:
  10.1 12.1 all-gather.12
  23.9 9.9 all-gather.14
  35.4 10.6 all-gather.16
  47.5 9.9 all-gather.18
where the time goes:
time: 137 us
  local copies, waits for them, and re-layouts  34.7 us (25%)
  other arithmetic  33.2 us (24%)
  starting transfers between devices  23.3 us (17%)
  between operations  15.2 us (11%)
  matrix products  15.1 us (11%)
  blocking collectives  9.69 us (7%)
  waiting for transfers between devices  5.66 us (4%)
    dot_general x4, matrix products, project_norm(): output = jnp.dot(hidden, second, preferred_element_type=jnp.float32)  14.1 us
    all_to_all x2, starting transfers between devices, per_device(): lax.all_to_all(packed, 'dom', split_axis=1, concat_axis=1, tiled=True)  11.8 us
    convert_element_type x2, other arithmetic, per_device(): new_edges = jnp.where(live_mask[None, :, None], edge_state.astype(jnp.flo...  9.73 us
    ppermute x2, starting transfers between devices, with_halo(): lax.ppermute(lax.slice_in_dim(block, 0, width, axis=dim), axis, backward)  9.32 us
    gather x2, local copies, waits for them, and re-layouts, per_device(): receiver_rows = jnp.take(node_state, edge_receivers, axis=1)  8 us
    select_n x3, other arithmetic, per_device(): receiver_rows = jnp.take(node_state, edge_receivers, axis=1)  7.59 us
    gather x2, local copies, waits for them, and re-layouts, per_device(): sender_rows = jnp.take(sources, edge_senders, axis=1)  7.11 us
    concatenate x2, other arithmetic, per_device(): joined = jnp.concatenate([edge_state, sender_rows, receiver_rows], -1)  6.59 us
  transfers between devices with their start and end apart: 10, of which 1 were waited for; matrix products, arithmetic and copies ran while one was open for 55% of the time, Pallas kernels for 0%

commit v1 on v0

v1 whole, which is shorter than its diff:
```python
import functools

import jax
import jax.numpy as jnp
from jax import lax
from jax.experimental import pallas as pl
from jax.experimental.pallas import tpu as pltpu
from jax.sharding import PartitionSpec as P

F32, BF16 = jnp.float32, jnp.bfloat16
LANES = 128
CHUNK = 256


def round_up(value, step):
    return (value + step - 1) // step * step


def dot(a, b):
    return jnp.dot(a, b, preferred_element_type=F32)


def silu(x):
    half = 0.5 * x
    return (half + half * jnp.tanh(half)).astype(BF16)


def norm(x, gain, shift):
    average = jnp.mean(x, -1, keepdims=True)
    centred = x - average
    variance = jnp.mean(centred * centred, -1, keepdims=True)
    return centred * lax.rsqrt(variance + 1e-05) * gain + shift


def kernel(
    sizes,
    node_in, edge_in, index_in, ef_in, es_in, nf_in, ns_in, eg_in, eb_in, ng_in, nb_in,
    node_out, edge_out,
    node, edge, index, w1, w2, w3, w4, eg, eb, ng, nb,
    gather, scatter, picker, table, near, pre, node_pre, summed,
    halo_out, halo, far_out, far, far_rows,
    local_sem, wl_sem, ws_sem, wr_sem, hs_sem, hr_sem, fs_sem, fr_sem,
):
    n, layers, members, nodes, edges, width, side_rows, slots, far_base = sizes
    me = lax.axis_index("dom")
    core = lax.axis_index("mem")
    halves = 2
    half = width // halves
    other = 1 - core

    barrier = pltpu.get_barrier_semaphore()
    pl.semaphore_signal(barrier, inc=1, device_id={"mem": other})
    for step in range(1, n):
        pl.semaphore_signal(barrier, inc=1, device_id={"dom": lax.rem(me + step, n)})

    loads = []
    for place, (src, dst) in enumerate(
        ((node_in, node), (index_in, index), (edge_in, edge), (eg_in, eg), (eb_in, eb), (ng_in, ng), (nb_in, nb))
    ):
        copy = pltpu.make_async_copy(src, dst, local_sem.at[place])
        copy.start()
        loads.append(copy)
    weights = ((ef_in, w1), (es_in, w2), (nf_in, w3), (ns_in, w4))
    own = {}
    for l in range(layers):
        for k, (src, dst) in enumerate(weights):
            own[l, k] = pltpu.make_async_copy(src.at[l], dst.at[l, core], wl_sem.at[l, k])
            own[l, k].start()

    loads[1].wait()
    depth = gather.shape[1]
    turned = jnp.transpose(jnp.broadcast_to(index[0:1, :], (LANES, index.shape[1])))
    senders = turned[:edges]
    receivers = turned[edges : 2 * edges] + nodes
    senders = jnp.where(senders < nodes, senders, senders + nodes)
    for c in range(depth // LANES):
        lane = lax.broadcasted_iota(jnp.int32, (edges, LANES), 1) + c * LANES
        gather[:, c * LANES : (c + 1) * LANES] = (
            ((senders == lane) | (receivers == lane)).astype(F32).astype(BF16)
        )
    row = lax.broadcasted_iota(jnp.int32, (nodes, edges), 0)
    scatter[...] = (
        (jnp.broadcast_to(index[0:1, edges : 2 * edges], (nodes, edges)) == row).astype(F32).astype(BF16)
    )
    pick_rows = picker.shape[0]
    base = 2 * edges + LANES
    for c in range(nodes // LANES):
        lane = lax.broadcasted_iota(jnp.int32, (pick_rows, LANES), 1) + c * LANES
        picker[:, c * LANES : (c + 1) * LANES] = (
            (turned[base : base + pick_rows] == lane).astype(F32).astype(BF16)
        )
    count = index[0:1, 2 * edges : 2 * edges + 1]
    for m in range(members):
        table[m, far_base:, :] = jnp.zeros((table.shape[1] - far_base, width), BF16)

    loads[0].wait()
    pending = []
    partner = {}
    for l in range(layers):
        for m in range(members):
            packed = dot(picker[...], node[m])
            for side in range(2):
                halo_out[l, side, m * side_rows : (m + 1) * side_rows, :] = packed[
                    side * side_rows : (side + 1) * side_rows
                ].astype(BF16)
            for q in range(n):
                start = 2 * side_rows + q * slots
                far_out[l, q, m * slots : (m + 1) * slots, :] = packed[start : start + slots].astype(BF16)
        if l == 0:
            pl.semaphore_wait(barrier, n)
        arrivals = []
        for side, step in ((1, 1), (0, n - 1)):
            copy = pltpu.make_async_remote_copy(
                src_ref=halo_out.at[l, side],
                dst_ref=halo.at[l, 1 - side],
                send_sem=hs_sem.at[l, side],
                recv_sem=hr_sem.at[l, side],
                device_id={"dom": lax.rem(me + step, n)},
            )
            copy.start()
            arrivals.append(copy)
        for step in range(1, n):
            target = lax.rem(me + step, n)
            copy = pltpu.make_async_remote_copy(
                src_ref=far_out.at[l, target],
                dst_ref=far.at[l, me],
                send_sem=fs_sem.at[l, step],
                recv_sem=fr_sem.at[l, step],
                device_id={"dom": target},
            )
            copy.start()
            arrivals.append(copy)
        mine = pltpu.make_async_copy(far_out.at[l, me], far.at[l, me], fr_sem.at[l, 0])
        mine.start()
        if l == 0:
            for ll in range(layers):
                for k, (src, dst) in enumerate(weights):
                    copy = pltpu.make_async_remote_copy(
                        src_ref=src.at[ll],
                        dst_ref=dst.at[ll, core],
                        send_sem=ws_sem.at[ll, k],
                        recv_sem=wr_sem.at[ll, k],
                        device_id={"mem": other},
                    )
                    copy.start()
                    partner[ll, k] = copy
                    pending.append(copy)
            loads[2].wait()
            for copy in loads[3:]:
                copy.wait()

        own[l, 0].wait()
        partner[l, 0].wait_recv()
        for h in range(halves):
            cols = slice(h * half, (h + 1) * half)
            stacked = node[...].reshape(members * nodes, width)
            by_sender = dot(stacked, w1[l, h, width : 2 * width, :]).astype(BF16)
            by_receiver = dot(stacked, w1[l, h, 2 * width :, :]).astype(BF16)
            for m in range(members):
                table[m, :nodes, cols] = by_sender[m * nodes : (m + 1) * nodes]
                table[m, nodes : 2 * nodes, cols] = by_receiver[m * nodes : (m + 1) * nodes]
        for m in range(members):
            for c in range(edges // CHUNK):
                rows = slice(c * CHUNK, (c + 1) * CHUNK)
                for h in range(halves):
                    cols = slice(h * half, (h + 1) * half)
                    pre[m, rows, cols] = dot(edge[m, rows, :], w1[l, h, :width, :]) + dot(
                        gather[rows, : 2 * nodes], table[m, : 2 * nodes, cols]
                    )
        own[l, 2].wait()
        partner[l, 2].wait_recv()
        for h in range(halves):
            cols = slice(h * half, (h + 1) * half)
            node_pre[:, cols] = dot(node[...].reshape(members * nodes, width), w3[l, h, :width, :])
        own[l, 1].wait()
        partner[l, 1].wait_recv()
        own[l, 3].wait()
        partner[l, 3].wait_recv()

        for copy in arrivals:
            copy.wait_recv()
        mine.wait()
        pending.extend(arrivals)
        for m in range(members):
            for side in range(2):
                near[m, side * side_rows : (side + 1) * side_rows, :] = halo[
                    l, side, m * side_rows : (m + 1) * side_rows, :
                ]
        for q in range(n):
            block = far[l, q].astype(F32)
            for m in range(members):
                far_rows[m, q * slots : (q + 1) * slots, :] = block[m * slots : (m + 1) * slots]
        for m in range(members):
            near[m, 2 * side_rows :, :] = far_rows[m].astype(BF16)
        count_near = near.shape[1]
        for h in range(halves):
            cols = slice(h * half, (h + 1) * half)
            moved = dot(near[...].reshape(members * count_near, width), w1[l, h, width : 2 * width, :]).astype(BF16)
            for m in range(members):
                table[m, 2 * nodes : 2 * nodes + count_near, cols] = moved[m * count_near : (m + 1) * count_near]

        for m in range(members):
            for c in range(edges // CHUNK):
                rows = slice(c * CHUNK, (c + 1) * CHUNK)
                hidden = silu(pre[m, rows, :] + dot(gather[rows, 2 * nodes :], table[m, 2 * nodes :, :]))
                out = jnp.concatenate([dot(hidden, w2[l, h]) for h in range(halves)], -1)
                update = norm(out, eg[l : l + 1, :], eb[l : l + 1, :])
                live = lax.broadcasted_iota(jnp.int32, (CHUNK, 1), 0) + c * CHUNK < count
                edge[m, rows, :] = jnp.where(live, edge[m, rows, :].astype(F32) + update, 0.0).astype(BF16)
            summed[m * nodes : (m + 1) * nodes, :] = dot(scatter[...], edge[m]).astype(BF16)
        if l == layers - 1:
            edge_store = pltpu.make_async_copy(edge, edge_out, local_sem.at[2])
            edge_store.start()

        first = jnp.concatenate(
            [
                node_pre[:, h * half : (h + 1) * half] + dot(summed[...], w3[l, h, width:, :])
                for h in range(halves)
            ],
            -1,
        )
        hidden = silu(first)
        out = jnp.concatenate([dot(hidden, w4[l, h]) for h in range(halves)], -1)
        update = norm(out, ng[l : l + 1, :], nb[l : l + 1, :])
        for m in range(members):
            node[m] = (node[m].astype(F32) + update[m * nodes : (m + 1) * nodes]).astype(BF16)
    node_store = pltpu.make_async_copy(node, node_out, local_sem.at[0])
    node_store.start()
    for copy in pending:
        copy.wait_send()
    edge_store.wait()
    node_store.wait()


def solution(mesh):
    n = mesh.shape["dom"]

    def step(
        node, edge, senders, receivers, counts, halo_send, long_send, ef, es, nf, ns, eg, eb, ng, nb
    ):
        members, nodes, width = node.shape
        edges = edge.shape[1]
        layers = ef.shape[0]
        side_rows = halo_send.shape[0] // 2
        slots = long_send.shape[-1]
        me = lax.axis_index("dom")
        sent = lax.dynamic_index_in_dim(long_send, me, 0, keepdims=False).reshape(-1)
        near_rows = 2 * side_rows + n * slots
        pick_rows = near_rows
        fill = round_up(pick_rows, LANES) - pick_rows
        index = jnp.concatenate(
            [senders, receivers, jnp.broadcast_to(counts, (LANES,)), halo_send, sent, jnp.zeros((fill,), jnp.int32)]
        ).reshape(1, -1)
        depth = 2 * nodes + round_up(near_rows, LANES)
        sizes = (n, layers, members, nodes, edges, width, side_rows, slots, 2 * nodes + near_rows)
        half = width // 2
        hbm = pl.BlockSpec(memory_space=pl.ANY)
        dma = pltpu.SemaphoreType.DMA
        return pl.pallas_call(
            functools.partial(kernel, sizes),
            out_shape=(
                jax.ShapeDtypeStruct(node.shape, BF16),
                jax.ShapeDtypeStruct(edge.shape, BF16),
            ),
            in_specs=[hbm] * 11,
            out_specs=(hbm, hbm),
            scratch_shapes=[
                pltpu.VMEM(node.shape, BF16),
                pltpu.VMEM(edge.shape, BF16),
                pltpu.VMEM(index.shape, jnp.int32),
                pltpu.VMEM((layers, 2, ef.shape[1], half), BF16),
                pltpu.VMEM((layers, 2, es.shape[1], half), BF16),
                pltpu.VMEM((layers, 2, nf.shape[1], half), BF16),
                pltpu.VMEM((layers, 2, ns.shape[1], half), BF16),
                pltpu.VMEM(eg.shape, F32),
                pltpu.VMEM(eb.shape, F32),
                pltpu.VMEM(ng.shape, F32),
                pltpu.VMEM(nb.shape, F32),
                pltpu.VMEM((edges, depth), BF16),
                pltpu.VMEM((nodes, edges), BF16),
                pltpu.VMEM((pick_rows, nodes), BF16),
                pltpu.VMEM((members, depth, width), BF16),
                pltpu.VMEM((members, near_rows, width), BF16),
                pltpu.VMEM((members, edges, width), F32),
                pltpu.VMEM((members * nodes, width), F32),
                pltpu.VMEM((members * nodes, width), BF16),
                pltpu.VMEM((layers, 2, members * side_rows, width), BF16),
                pltpu.VMEM((layers, 2, members * side_rows, width), BF16),
                pltpu.VMEM((layers, n, members * slots, width), BF16),
                pltpu.VMEM((layers, n, members * slots, width), BF16),
                pltpu.VMEM((members, n * slots, width), F32),
                dma((7,)),
                dma((layers, 4)),
                dma((layers, 4)),
                dma((layers, 4)),
                dma((layers, 2)),
                dma((layers, 2)),
                dma((layers, n)),
                dma((layers, n)),
            ],
            compiler_params=pltpu.CompilerParams(
                collective_id=0, has_side_effects=True, vmem_limit_bytes=56 * 1024 * 1024
            ),
        )(node, edge, index, ef, es, nf, ns, eg, eb, ng, nb)

    placed = (
        P("mem", "dom", None),
        P("mem", "dom", None),
        P("dom"),
        P("dom"),
        P("dom"),
        P("dom"),
        P(),
        P(None, None, "mem"),
        P(None, None, "mem"),
        P(None, None, "mem"),
        P(None, None, "mem"),
        P(),
        P(),
        P(),
        P(),
    )
    return jax.shard_map(
        step,
        mesh=mesh,
        in_specs=placed,
        out_specs=(P("mem", "dom", None), P("mem", "dom", None)),
        check_vma=False,
    )
```

time: 137 us -> 32.4 us (0.24)
  other arithmetic: 33.2 us -> 0 us
  local copies, waits for them, and re-layouts: 34.7 us -> 5.53 us
  Pallas kernels: 0 us -> 25.3 us
  starting transfers between devices: 23.3 us -> 0 us
  matrix products: 15.1 us -> 0 us
  between operations: 15.2 us -> 1.33 us
  blocking collectives: 9.69 us -> 0 us
  waiting for transfers between devices: 5.66 us -> 0 us
    pallas_call x0 -> x1, Pallas kernels: none -> 25.3 us  [step(): pl.pallas_call(functools.partial(kernel, sizes), out_shape=(jax.ShapeDtyp...]
    gather x9 -> x0, local copies, waits for them, and re-layouts: 18.2 us -> none  [the longest x2 8 us: per_device(): receiver_rows = jnp.take(node_state, edge_receivers, axis=1)]
    dot_general x6 -> x0, matrix products: 15.1 us -> none  [the longest x4 14.1 us: project_norm(): output = jnp.dot(hidden, second, preferred_element_type=jnp.float32)]
    select_n x12 -> x0, other arithmetic: 12.5 us -> none  [the longest x3 7.59 us: per_device(): receiver_rows = jnp.take(node_state, edge_receivers, axis=1)]
    all_to_all x2 -> x0, starting transfers between devices: 11.8 us -> none  [per_device(): lax.all_to_all(packed, 'dom', split_axis=1, concat_axis=1, tiled=True)]
    ppermute x4 -> x0, starting transfers between devices: 11.3 us -> none  [the longest x2 9.32 us: with_halo(): lax.ppermute(lax.slice_in_dim(block, 0, width, axis=dim), axis, backward)]
    convert_element_type x4 -> x0, other arithmetic: 9.85 us -> none  [the longest x2 9.73 us: per_device(): new_edges = jnp.where(live_mask[None, :, None], edge_state.astype(jnp.flo...]
    all_gather x4 -> x0, blocking collectives: 9.69 us -> none  [the longest x2 4.93 us: per_device(): lax.all_gather(node_second[layer_index], 'mem', axis=1, tiled=True)]
  transfers between devices with their start and end apart: 10 -> 0, of which waited for: 1 -> 0; matrix products, arithmetic and copies ran while one was open for 55% -> 0% of each run, Pallas kernels for 0% -> 0%
where the time goes in v1:
time: 32.4 us; the launch traced here: 32.1 us
  Pallas kernels  25.3 us (78%)
  local copies, waits for them, and re-layouts  5.53 us (17%)
  between operations  1.33 us (4%)
    pallas_call x1, Pallas kernels, step(): pl.pallas_call(functools.partial(kernel, sizes), out_shape=(jax.ShapeDtyp...  25.3 us
    unnamed x4, local copies, waits for them, and re-layouts  3.98 us
    concatenate x1, local copies, waits for them, and re-layouts, step(): jnp.concatenate([senders, receivers, jnp.broadcast_to(counts, (LANES,)),...  0.78 us

profile of v1, /device:TPU:0, one launch (start us, length us, event | category | flops | bytes accessed | tf_op | source)
XLA Modules:
  0.0 32.1 jit_solution(11752498381931823690)
XLA Ops:
  0.6 0.0 copy-start
  1.3 0.0 copy-done
  1.4 0.1 copy.18
  1.4 0.1 reshape.11
  1.5 0.8 %concatenate.3 = s32[1280]{0:T(1024)S(1)} concatenate(s32[512]{0:T(512)} %param.17, s32[512]{0:T(512)} %param.18, s32[128]{0:T(128)S(1)} %broadcast_in_dim.11, s32[32]{0:T(128)} %param.20, s32[32]{0:T(128)S(1)} %reshape.11, s32[64]{0:T(128)S(1)} %broadcast_in_dim.12), dimensions={0} | concatenate | bytes 10240 | tf_op jit(solution)/shard_map/concatenate | solution.py:251
  2.3 0.6 %reshape.12.index_in = s32[1,1280]{1,0:T(1,128)} reshape(s32[1280]{0:T(1024)S(1)} %concatenate.3) | data formatting | bytes 10240 | tf_op jit(solution)/shard_map/reshape | solution.py:253
  2.9 25.3 %shard_map.158 = (bf16[2,128,512]{2,1,0:T(8,128)(2,1)}, bf16[2,512,512]{2,1,0:T(8,128)(2,1)}) custom-call(bf16[2,128,512]{2,1,0:T(8,128)(2,1)} %node_in.1, bf16[2,512,512]{2,1,0:T(8,128)(2,1)} %edge_in.1, s32[1,1280]{1,0:T(1,128)} %reshape.12.index_in, bf16[2,1536,256]{2,1,0:T(8,128)(2,1)} %ef_in.1, bf16[2,512,256]{2,1,0:T(8,128)(2,1)} %es_in.1, ...), custom_call_target="tpu_custom_call" | custom-call | tf_op jit(solution)/shard_map/pallas_call | solution.py:259
  28.2 1.7 %copy.22 = bf16[2,128,512]{2,1,0:T(8,128)(2,1)} copy(bf16[2,128,512]{2,1,0:T(8,128)(2,1)} %get-tuple-element.4) | data formatting | bytes 524288
  29.9 2.3 %copy.23 = bf16[2,512,512]{2,1,0:T(8,128)(2,1)} copy(bf16[2,512,512]{2,1,0:T(8,128)(2,1)} %get-tuple-element.5) | data formatting | bytes 2097152
  (3 shorter events, 0.0 us)
Async XLA Ops:
  0.6 0.7 %copy-start = (s32[16,16,2]{1,2,0:T(2,128)S(1)}, s32[16,16,2]{1,2,0:T(2,128)}, u32[]{:S(2)}) copy-start(s32[16,16,2]{1,2,0:T(2,128)} %param.21) | copy-start | bytes 6148

commit v2 on v0

v2 whole, which is shorter than its diff:
```python
import functools

import jax
import jax.numpy as jnp
from jax import lax
from jax.experimental import pallas as pl
from jax.experimental.pallas import tpu as pltpu
from jax.sharding import PartitionSpec as P

F32, BF16 = jnp.float32, jnp.bfloat16
LANES = 128
CHUNK = 256


def round_up(value, step):
    return (value + step - 1) // step * step


def dot(a, b):
    return jnp.dot(a, b, preferred_element_type=F32)


def silu(x):
    half = 0.5 * x
    return (half + half * jnp.tanh(half)).astype(BF16)


def norm(x, gain, shift):
    average = jnp.mean(x, -1, keepdims=True)
    centred = x - average
    variance = jnp.mean(centred * centred, -1, keepdims=True)
    return centred * lax.rsqrt(variance + 1e-05) * gain + shift


def edge_update(m, edges, refs):
    edge, pre, table, gather, scatter, w2, eg, eb, count, split = refs
    halves = pre.shape[0]
    for c in range(edges // CHUNK):
        rows = slice(c * CHUNK, (c + 1) * CHUNK)
        hidden = jnp.concatenate(
            [silu(pre[h, m, rows, :] + dot(gather[rows, split:], table[h, m, split:, :])) for h in range(halves)], -1
        )
        out = jnp.concatenate([dot(hidden, w2[h]) for h in range(halves)], -1)
        update = norm(out, eg, eb)
        live = lax.broadcasted_iota(jnp.int32, (CHUNK, 1), 0) + c * CHUNK < count
        edge[m, rows, :] = jnp.where(live, edge[m, rows, :].astype(F32) + update, 0.0).astype(BF16)
    return dot(scatter[...], edge[m]).astype(BF16)


def node_update(m, summed, refs):
    node, node_pre, w3, w4, ng, nb = refs
    halves, half = w4.shape[0], w4.shape[2]
    width = half * halves
    hidden = jnp.concatenate(
        [silu(node_pre[h, m] + dot(summed, w3[h, width:, :])) for h in range(halves)], -1
    )
    out = jnp.concatenate([dot(hidden, w4[h]) for h in range(halves)], -1)
    node[m] = (node[m].astype(F32) + norm(out, ng, nb)).astype(BF16)


def exchange_kernel(
    sizes,
    node_in, edge_in, senders_in, receivers_in, counts_in, halo_in, long_in,
    ef_in, es_in, nf_in, ns_in, eg_in, eb_in, ng_in, nb_in,
    node, edge, pre, node_pre, table, gather, scatter, w2, w3, w4, eg, eb, ng, nb, count_row,
    w1, senders_v, receivers_v, count_s, halo_v, long_v, picked, picker, near, far_rows,
    halo_out, halo, far_out, far,
    local_sem, wl_sem, ws_sem, wr_sem, hs_sem, hr_sem, fs_sem, fr_sem,
):
    n, layers, members, nodes, edges, width, side_rows, slots = sizes
    me = lax.axis_index("dom")
    core = lax.axis_index("mem")
    halves = 2
    other = 1 - core
    split = 2 * nodes

    barrier = pltpu.get_barrier_semaphore()
    pl.semaphore_signal(barrier, inc=1, device_id={"mem": other})
    for step in range(1, n):
        pl.semaphore_signal(barrier, inc=1, device_id={"dom": lax.rem(me + step, n)})

    loads = []
    for place, (src, dst) in enumerate((
        (node_in, node), (halo_in, halo_v), (long_in.at[me], long_v), (senders_in, senders_v),
        (receivers_in, receivers_v), (counts_in, count_s), (edge_in, edge),
        (eg_in, eg), (eb_in, eb), (ng_in, ng), (nb_in, nb),
    )):
        copy = pltpu.make_async_copy(src, dst, local_sem.at[place])
        loads.append(copy)
    weights = ((ef_in, w1), (es_in, w2), (nf_in, w3), (ns_in, w4))
    own = {}
    for l in range(layers):
        for k, (src, dst) in enumerate(weights):
            own[l, k] = pltpu.make_async_copy(src.at[l], dst.at[l, core], wl_sem.at[l, k])
    for copy in loads[:6]:
        copy.start()
    own[0, 0].start()
    loads[6].start()
    for place in loads[7:]:
        place.start()
    for key in own:
        if key != (0, 0):
            own[key].start()

    def column(row):
        wide = round_up(row.shape[1], LANES)
        if wide > row.shape[1]:
            row = jnp.concatenate([row, jnp.zeros((1, wide - row.shape[1]), jnp.int32)], 1)
        return jnp.transpose(jnp.broadcast_to(row, (LANES, wide)))

    def one_hot(hits):
        return hits.astype(F32).astype(BF16)

    loads[1].wait()
    loads[2].wait()
    picked[: 2 * side_rows, :] = column(halo_v[...].reshape(1, 2 * side_rows))[: 2 * side_rows]
    for s in range(slots):
        picked[pl.ds(2 * side_rows + s, n, stride=slots), :] = column(long_v[s : s + 1, :])[:n]
    for c in range(nodes // LANES):
        lane = lax.broadcasted_iota(jnp.int32, picked.shape, 1) + c * LANES
        picker[:, c * LANES : (c + 1) * LANES] = one_hot(picked[...] == lane)

    pending = []
    arrivals = {}

    def send(l, m):
        packed = dot(picker[...], node[m])
        for side in range(2):
            halo_out[l, m, side] = packed[side * side_rows : (side + 1) * side_rows].astype(BF16)
        for q in range(n):
            start = 2 * side_rows + q * slots
            far_out[l, m, q] = packed[start : start + slots].astype(BF16)
        if l == 0 and m == 0:
            pl.semaphore_wait(barrier, n)
        copies = []
        for step in range(1, n):
            target = lax.rem(me + step, n)
            copies.append(pltpu.make_async_remote_copy(
                src_ref=far_out.at[l, m, target],
                dst_ref=far.at[l, m, me],
                send_sem=fs_sem.at[l, m, step],
                recv_sem=fr_sem.at[l, m, step],
                device_id={"dom": target},
            ))
        for side, step in ((1, 1), (0, n - 1)):
            copies.append(pltpu.make_async_remote_copy(
                src_ref=halo_out.at[l, m, side],
                dst_ref=halo.at[l, m, 1 - side],
                send_sem=hs_sem.at[l, m, side],
                recv_sem=hr_sem.at[l, m, side],
                device_id={"dom": lax.rem(me + step, n)},
            ))
        for copy in copies:
            copy.start()
        mine = pltpu.make_async_copy(far_out.at[l, m, me], far.at[l, m, me], fr_sem.at[l, m, 0])
        mine.start()
        pending.extend(copies)
        arrivals[l, m] = (copies, mine)

    def prepare(l, h, ms):
        for m in ms:
            table[h, m, :nodes, :] = dot(node[m], w1[l, h, width : 2 * width, :]).astype(BF16)
            table[h, m, nodes:split, :] = dot(node[m], w1[l, h, 2 * width :, :]).astype(BF16)
        for m in ms:
            pre[h, m] = dot(edge[m], w1[l, h, :width, :]) + dot(gather[:, :split], table[h, m, :split, :])

    def node_prepare(l, m):
        for h in range(halves):
            node_pre[h, m] = dot(node[m], w3[l, h, :width, :])

    def receive(l, m):
        copies, mine = arrivals[l, m]
        for copy in copies:
            copy.wait_recv()
        mine.wait()
        for side in range(2):
            near[m, side * side_rows : (side + 1) * side_rows, :] = halo[l, m, side]
        for q in range(n):
            far_rows[m, q * slots : (q + 1) * slots, :] = far[l, m, q].astype(F32)
        near[m, 2 * side_rows :, :] = far_rows[m].astype(BF16)
        count_near = near.shape[1]
        for h in range(halves):
            table[h, m, split : split + count_near, :] = dot(near[m], w1[l, h, width : 2 * width, :]).astype(BF16)

    loads[0].wait()
    for m in range(members):
        send(0, m)
    partner = {}
    for l in range(layers):
        for k, (src, dst) in enumerate(weights):
            copy = pltpu.make_async_remote_copy(
                src_ref=src.at[l],
                dst_ref=dst.at[l, core],
                send_sem=ws_sem.at[l, k],
                recv_sem=wr_sem.at[l, k],
                device_id={"mem": other},
            )
            copy.start()
            partner[l, k] = copy
            pending.append(copy)

    loads[3].wait()
    loads[4].wait()
    depth = gather.shape[1]
    senders = column(senders_v[...].reshape(1, edges))
    receiver_row = receivers_v[...].reshape(1, edges)
    receivers = column(receiver_row) + nodes
    senders = jnp.where(senders < nodes, senders, senders + nodes)
    for c in range(depth // LANES):
        lane = lax.broadcasted_iota(jnp.int32, (edges, LANES), 1) + c * LANES
        gather[:, c * LANES : (c + 1) * LANES] = one_hot((senders == lane) | (receivers == lane))
    row = lax.broadcasted_iota(jnp.int32, (nodes, edges), 0)
    scatter[...] = one_hot(jnp.broadcast_to(receiver_row, (nodes, edges)) == row)
    far_base = split + near.shape[1]
    if far_base < depth:
        for h in range(halves):
            for m in range(members):
                table[h, m, far_base:, :] = jnp.zeros((depth - far_base, table.shape[3]), BF16)
    loads[5].wait()
    count_row[...] = jnp.full(count_row.shape, count_s[0], jnp.int32)
    for copy in loads[6:]:
        copy.wait()
    own[0, 0].wait()
    everyone = range(members)
    prepare(0, core, everyone)
    partner[0, 0].wait_recv()
    prepare(0, other, everyone)
    for k in (1, 2, 3):
        own[0, k].wait()
        partner[0, k].wait_recv()
    for m in everyone:
        node_prepare(0, m)

    for l in range(layers):
        if l > 0:
            own[l, 0].wait()
            partner[l, 0].wait_recv()
            for h in range(halves):
                prepare(l, h, everyone)
            for k in (1, 2, 3):
                own[l, k].wait()
                partner[l, k].wait_recv()
            for m in everyone:
                node_prepare(l, m)
        for m in everyone:
            receive(l, m)
            if l == layers - 1 and m == members - 1:
                continue
            summed = edge_update(m, edges, (
                edge, pre, table, gather, scatter, w2.at[l], eg[l : l + 1, :], eb[l : l + 1, :],
                count_row[0:1, 0:1], split,
            ))
            node_update(m, summed, (node, node_pre, w3.at[l], w4.at[l], ng[l : l + 1, :], nb[l : l + 1, :]))
            if l < layers - 1:
                send(l + 1, m)
    for copy in pending:
        copy.wait_send()


def finish_kernel(
    sizes,
    node, edge, pre, node_pre, table, gather, scatter, w2, w3, w4, eg, eb, ng, nb, count_row,
    node_out, edge_out, edge_new, node_new, sem,
):
    n, layers, members, nodes, edges, width, side_rows, slots = sizes
    l, m = layers - 1, members - 1
    copies = []

    def store(src, dst):
        copy = pltpu.make_async_copy(src, dst, sem.at[len(copies)])
        copy.start()
        copies.append(copy)

    store(edge.at[:m], edge_out.at[:m])
    store(node.at[:m], node_out.at[:m])
    halves = pre.shape[0]
    split = 2 * nodes
    total = None
    count = count_row[0:1, 0:1]
    for c in range(edges // CHUNK):
        rows = slice(c * CHUNK, (c + 1) * CHUNK)
        hidden = jnp.concatenate(
            [silu(pre[h, m, rows, :] + dot(gather[rows, split:], table[h, m, split:, :])) for h in range(halves)], -1
        )
        out = jnp.concatenate([dot(hidden, w2[l, h]) for h in range(halves)], -1)
        update = norm(out, eg[l : l + 1, :], eb[l : l + 1, :])
        live = lax.broadcasted_iota(jnp.int32, (CHUNK, 1), 0) + c * CHUNK < count
        edge_new[rows, :] = jnp.where(live, edge[m, rows, :].astype(F32) + update, 0.0).astype(BF16)
        store(edge_new.at[rows], edge_out.at[m, rows])
    summed = dot(scatter[...], edge_new[...]).astype(BF16)
    hidden = jnp.concatenate(
        [silu(node_pre[h, m] + dot(summed, w3[l, h, width:, :])) for h in range(halves)], -1
    )
    out = jnp.concatenate([dot(hidden, w4[l, h]) for h in range(halves)], -1)
    update = norm(out, ng[l : l + 1, :], nb[l : l + 1, :])
    node_new[...] = (node[m].astype(F32) + update).astype(BF16)
    store(node_new, node_out.at[m])
    for copy in copies:
        copy.wait()


def solution(mesh):
    n = mesh.shape["dom"]

    def step(
        node, edge, senders, receivers, counts, halo_send, long_send, ef, es, nf, ns, eg, eb, ng, nb
    ):
        members, nodes, width = node.shape
        edges = edge.shape[1]
        layers = ef.shape[0]
        side_rows = halo_send.shape[0] // 2
        slots = long_send.shape[-1]
        long_rows = jnp.swapaxes(long_send, 1, 2)
        near_rows = 2 * side_rows + n * slots
        depth = 2 * nodes + round_up(near_rows, LANES)
        sizes = (n, layers, members, nodes, edges, width, side_rows, slots)
        half = width // 2
        hbm = pl.BlockSpec(memory_space=pltpu.HBM)
        vmem = pl.BlockSpec(memory_space=pltpu.VMEM)
        dma = pltpu.SemaphoreType.DMA
        kept = [
            (node.shape, BF16),
            (edge.shape, BF16),
            ((2, members, edges, half), F32),
            ((2, members, nodes, half), F32),
            ((2, members, depth, half), BF16),
            ((edges, depth), BF16),
            ((nodes, edges), BF16),
            ((layers, 2, es.shape[1], half), BF16),
            ((layers, 2, nf.shape[1], half), BF16),
            ((layers, 2, ns.shape[1], half), BF16),
            (eg.shape, F32),
            (eb.shape, F32),
            (ng.shape, F32),
            (nb.shape, F32),
            ((1, LANES), jnp.int32),
        ]
        state = pl.pallas_call(
            functools.partial(exchange_kernel, sizes),
            out_shape=tuple(pltpu.VMEM(shape, kind) for shape, kind in kept),
            in_specs=[hbm] * 15,
            out_specs=(vmem,) * len(kept),
            scratch_shapes=[
                pltpu.VMEM((layers, 2, ef.shape[1], half), BF16),
                pltpu.VMEM(senders.shape, jnp.int32),
                pltpu.VMEM(receivers.shape, jnp.int32),
                pltpu.SMEM(counts.shape, jnp.int32),
                pltpu.VMEM(halo_send.shape, jnp.int32),
                pltpu.VMEM(long_rows.shape[1:], jnp.int32),
                pltpu.VMEM((near_rows, LANES), jnp.int32),
                pltpu.VMEM((near_rows, nodes), BF16),
                pltpu.VMEM((members, near_rows, width), BF16),
                pltpu.VMEM((members, n * slots, width), F32),
                pltpu.VMEM((layers, members, 2, side_rows, width), BF16),
                pltpu.VMEM((layers, members, 2, side_rows, width), BF16),
                pltpu.VMEM((layers, members, n, slots, width), BF16),
                pltpu.VMEM((layers, members, n, slots, width), BF16),
                dma((11,)),
                dma((layers, 4)),
                dma((layers, 4)),
                dma((layers, 4)),
                dma((layers, members, 2)),
                dma((layers, members, 2)),
                dma((layers, members, n)),
                dma((layers, members, n)),
            ],
            compiler_params=pltpu.CompilerParams(
                collective_id=0, has_side_effects=True, vmem_limit_bytes=51 * 1024 * 1024
            ),
        )(node, edge, senders, receivers, counts, halo_send, long_rows, ef, es, nf, ns, eg, eb, ng, nb)
        return pl.pallas_call(
            functools.partial(finish_kernel, sizes),
            out_shape=(
                jax.ShapeDtypeStruct(node.shape, BF16),
                jax.ShapeDtypeStruct(edge.shape, BF16),
            ),
            in_specs=[vmem] * len(kept),
            out_specs=(hbm, hbm),
            scratch_shapes=[
                pltpu.VMEM((edges, width), BF16),
                pltpu.VMEM((nodes, width), BF16),
                dma((3 + edges // CHUNK,)),
            ],
            compiler_params=pltpu.CompilerParams(vmem_limit_bytes=40 * 1024 * 1024),
        )(*state)

    placed = (
        P("mem", "dom", None),
        P("mem", "dom", None),
        P("dom"),
        P("dom"),
        P("dom"),
        P("dom"),
        P(),
        P(None, None, "mem"),
        P(None, None, "mem"),
        P(None, None, "mem"),
        P(None, None, "mem"),
        P(),
        P(),
        P(),
        P(),
    )
    return jax.shard_map(
        step,
        mesh=mesh,
        in_specs=placed,
        out_specs=(P("mem", "dom", None), P("mem", "dom", None)),
        check_vma=False,
    )
```

time: 137 us -> 26.9 us (0.20)
  local copies, waits for them, and re-layouts: 34.7 us -> 0 us
  other arithmetic: 33.2 us -> 0 us
  Pallas kernels: 0 us -> 25.5 us
  starting transfers between devices: 23.3 us -> 0 us
  matrix products: 15.1 us -> 0 us
  between operations: 15.2 us -> 1.29 us
  blocking collectives: 9.69 us -> 0 us
  waiting for transfers between devices: 5.66 us -> 0 us
    pallas_call x0 -> x2, Pallas kernels: none -> 25.5 us  [the longest x1 23 us: step(): pl.pallas_call(functools.partial(exchange_kernel, sizes), out_shape=tuple...]
    gather x9 -> x0, local copies, waits for them, and re-layouts: 18.2 us -> none  [the longest x2 8 us: per_device(): receiver_rows = jnp.take(node_state, edge_receivers, axis=1)]
    dot_general x6 -> x0, matrix products: 15.1 us -> none  [the longest x4 14.1 us: project_norm(): output = jnp.dot(hidden, second, preferred_element_type=jnp.float32)]
    select_n x12 -> x0, other arithmetic: 12.5 us -> none  [the longest x3 7.59 us: per_device(): receiver_rows = jnp.take(node_state, edge_receivers, axis=1)]
    all_to_all x2 -> x0, starting transfers between devices: 11.8 us -> none  [per_device(): lax.all_to_all(packed, 'dom', split_axis=1, concat_axis=1, tiled=True)]
    ppermute x4 -> x0, starting transfers between devices: 11.3 us -> none  [the longest x2 9.32 us: with_halo(): lax.ppermute(lax.slice_in_dim(block, 0, width, axis=dim), axis, backward)]
    convert_element_type x4 -> x0, other arithmetic: 9.85 us -> none  [the longest x2 9.73 us: per_device(): new_edges = jnp.where(live_mask[None, :, None], edge_state.astype(jnp.flo...]
    all_gather x4 -> x0, blocking collectives: 9.69 us -> none  [the longest x2 4.93 us: per_device(): lax.all_gather(node_second[layer_index], 'mem', axis=1, tiled=True)]
  transfers between devices with their start and end apart: 10 -> 0, of which waited for: 1 -> 0; matrix products, arithmetic and copies ran while one was open for 55% -> 0% of each run, Pallas kernels for 0% -> 0%
where the time goes in v2:
time: 26.9 us; the launch traced here: 26.8 us
  Pallas kernels  25.5 us (95%)
  between operations  1.29 us (5%)
    pallas_call x1, Pallas kernels, step(): pl.pallas_call(functools.partial(exchange_kernel, sizes), out_shape=tuple...  23 us
    pallas_call x1, Pallas kernels, step(): pl.pallas_call(functools.partial(finish_kernel, sizes), out_shape=(jax.Sh...  2.53 us

profile of v2, /device:TPU:0, one launch (start us, length us, event | category | flops | bytes accessed | tf_op | source)
XLA Modules:
  0.0 26.8 jit_solution(4181625288004939609)
XLA Ops:
  1.3 23.0 %shard_map.158 = (bf16[2,128,512]{2,1,0:T(8,128)(2,1)S(1)}, bf16[2,512,512]{2,1,0:T(8,128)(2,1)S(1)}, f32[2,2,512,256]{3,2,1,0:T(8,128)S(1)}, f32[2,2,128,256]{3...) custom-call(bf16[2,128,512]{2,1,0:T(8,128)(2,1)} %node_in.1, ...), custom_call_target="tpu_custom_call" | custom-call | tf_op jit(solution)/shard_map/pallas_call | solution.py:338
  24.2 2.5 %shard_map.159 = (bf16[2,128,512]{2,1,0:T(8,128)(2,1)}, bf16[2,512,512]{2,1,0:T(8,128)(2,1)}) custom-call(bf16[2,128,512]{2,1,0:T(8,128)(2,1)S(1)} %get-tuple-element.17.node, bf16[2,512,512]{2,1,0:T(8,128)(2,1)S(1)} %get-tuple-element.18.edge, f32[2,2,512,256]{3,2,1,0:T(8,128)S(1)} %get-tuple-element.19.pre, ...), custom_call_target="tpu_custom_call" | custom-call | tf_op jit(solution)/shard_map/pallas_call | solution.py:371
